TPU v7x, 8 devices: a whole 2x2x1 slice. The times are simulated.
8 devices in a mesh: dp: 1 (over z), a: 2 (over y), b: 4 (over x, core).
Axes of the slice: x: 2, y: 2, z: 1, core: 2. Of those that a mesh axis runs over, the one named last changes fastest.
Arguments:
- x: bfloat16 [2048, 12288], P('dp', ('a', 'b'))
- w_gate: bfloat16 [12288, 33792], P('a', 'b')
- w_up: bfloat16 [12288, 33792], P('a', 'b')
- w_down: bfloat16 [33792, 12288], P('b', 'a')
Outputs:
- output: bfloat16 [2048, 12288], P('dp', ('a', 'b'))
All inputs are finite; a program needn't handle non-finite values.
Results may differ from a plain program's by a relative error of at most 0.016.
Values are sent between devices in bfloat16 or wider.
A program may use at most 2 GiB of HBM per device.

v0:
```python
import jax
import jax.numpy as jnp


def solution(mesh):
    def step(x, w_gate, w_up, w_down):
        gate, up = jnp.dot(x, w_gate), jnp.dot(x, w_up)
        hidden = (jax.nn.silu(gate.astype(jnp.float32)) * up.astype(jnp.float32)).astype(jnp.bfloat16)
        return jnp.dot(hidden, w_down)

    return step
```

profile of v0, /device:TPU:0, one launch (start us, length us, event | category | flops | bytes accessed | tf_op | source)
XLA Modules:
  0.0 2532.3 jit_solution(1275489821112119021)
XLA Ops:
  6.5 0.0 all-gather.4.cloned.1.call-start
  6.5 0.7 all-gather.4.cloned.1.call-update
  7.3 0.0 all-reduce.7.cloned.1.call-start
  7.3 157.3 %all-gather.4.cloned.1.call-done = bf16[2048,6144]{1,0:T(8,128)(2,1)} async-done(((bf16[2048,1536]{1,0:T(8,128)(2,1)}), bf16[2048,6144]{1,0:T(8,128)(2,1)}) %all-gather.4.cloned.1.call-update) | async-done | bytes 25165840 | tf_op args[0]
  164.6 226.3 %fusion.9 = bf16[2048,8448]{1,0:T(8,128)(2,1)} fusion(bf16[2048,6144]{1,0:T(8,128)(2,1)} %all-gather.4.cloned.1.call-done, bf16[6144,8448]{1,0:T(8,128)(2,1)} %param.2), kind=kOutput, calls=%fused_computation.10 | convolution fusion | flops 212600881152 | bytes 163577856 | tf_op jit(solution)/dot_general | solution.py:7
  390.8 226.2 %fusion.8 = bf16[2048,8448]{1,0:T(8,128)(2,1)} fusion(bf16[2048,6144]{1,0:T(8,128)(2,1)} %all-gather.4.cloned.1.call-done, bf16[6144,8448]{1,0:T(8,128)(2,1)} %param.1), kind=kOutput, calls=%fused_computation.9 | convolution fusion | flops 212600881152 | bytes 163577856 | tf_op jit(solution)/dot_general | solution.py:7
  617.0 0.0 all-reduce.7.cloned.1.call-update
  617.1 0.0 reduce-scatter.4.cloned.1.call-start
  617.1 1496.0 %all-reduce.7.cloned.1.call-done = (bf16[2048,8448]{1,0:T(8,128)(2,1)}, bf16[2048,8448]{1,0:T(8,128)(2,1)}) async-done(((bf16[2048,8448]{1,0:T(8,128)(2,1)}, bf16[2048,8448]{1,0:T(8,128)(2,1)}), (bf16[2048,8448]{1,0:T(8,128)(2,1)}, bf16[2048,8448]{1,0:T(8,128)(2,1)})) %all-reduce.7.cloned.1.call-update) | async-done | bytes 69206032 | tf_op jit(solution)/dot_general | solution.py:7
  2113.1 241.4 %fusion.5 = bf16[2048,6144]{1,0:T(8,128)(2,1)} fusion(bf16[8448,6144]{1,0:T(8,128)(2,1)} %param.3, bf16[2048,8448]{1,0:T(8,128)(2,1)} %get-tuple-element.4, bf16[2048,8448]{1,0:T(8,128)(2,1)} %get-tuple-element.5), kind=kOutput, calls=%fused_computation.7 | convolution fusion | flops 212739293184 | bytes 198180864 | tf_op jit(solution)/dot_general | solution.py:9
  2354.4 0.0 reduce-scatter.4.cloned.1.call-update
  2354.5 171.3 %reduce-scatter.4.cloned.1.call-done = bf16[2048,1536]{1,0:T(8,128)(2,1)} async-done(((bf16[2048,6144]{1,0:T(8,128)(2,1)}), bf16[2048,1536]{1,0:T(8,128)(2,1)}) %reduce-scatter.4.cloned.1.call-update) | async-done | bytes 6291472
Async XLA Ops:
  6.5 158.0 %all-gather.4.cloned.1.call-start = ((), (), s32[]{:S(2)}) async-start(), calls=%async_computation.1 | async-start | bytes 31457280 | tf_op args[0]
  7.3 2105.8 %all-reduce.7.cloned.1.call-start = ((), (), s32[]{:S(2)}) async-start(), calls=%async_computation.3 | async-start | bytes 138412032 | tf_op jit(solution)/dot_general | solution.py:7
  617.1 1908.7 %reduce-scatter.4.cloned.1.call-start = ((), (), s32[]{:S(2)}) async-start(), calls=%async_computation.2 | async-start | bytes 31457280
Sparse Core Ops, SparseCore 0:
  8.9 155.6 all-gather.3
  617.2 1495.8 all-reduce.6
  2354.6 171.1 reduce-scatter.3
where the time goes:
time: 2530 us
  waiting for transfers between devices  1830 us (72%)
  matrix products  694 us (27%)
    dot_general x1, waiting for transfers between devices, step(): gate, up = (jnp.dot(x, w_gate), jnp.dot(x, w_up))  1500 us
    dot_general x2, matrix products, step(): gate, up = (jnp.dot(x, w_gate), jnp.dot(x, w_up))  452 us
    unnamed x5, waiting for transfers between devices  329 us
    dot_general x1, matrix products, step(): return jnp.dot(hidden, w_down)  241 us
  transfers between devices with their start and end apart: 3, of which 3 were waited for; matrix products, arithmetic and copies ran while one was open for 0% of the time, Pallas kernels for 0%

commit v1 on v0

v1 whole, which is shorter than its diff:
```python
import functools
import jax
import jax.numpy as jnp
from jax import lax
from jax.experimental import pallas as pl
from jax.experimental.pallas import tpu as pltpu
from jax.sharding import PartitionSpec as P

R = 256
F = 256
GROUP = 3
LAG_HIDDEN = 4
LAG_DOWN = 12
SLOTS = LAG_DOWN + 2
HSLOTS = LAG_DOWN // GROUP + 1
WSLOTS = 2
VMEM_LIMIT = 66 * 1000 * 1000


def kernel(x, w_gate, w_up, w_down, y, xg, xv, wg, wu, wd, acc, own, keep, sent, got, hid, rsent, rgot, yout,
           x_send, x_recv, x_load, wg_sem, wu_sem, wd_sem, p_send, p_recv, h_send, h_recv, r_send, r_recv, y_sem):
    dp, a, b = lax.axis_index("dp"), lax.axis_index("a"), lax.axis_index("b")
    nb = 4
    half = R // 2
    rows, xb = x.shape
    ff, dn = w_down.shape
    chunks, tiles = rows // R, ff // F
    steps = chunks * tiles
    third, sub = dn // GROUP, acc.shape[2]
    depth = F * GROUP
    down_groups = tiles // GROUP
    lag_sum = (2 * tiles) // 3
    mesh_id = pltpu.DeviceIdType.MESH if hasattr(pltpu, "DeviceIdType") else pl.DeviceIdType.MESH
    partner = (dp, 1 - a, b)

    def peer(o):
        return lax.rem(b + o, nb)

    def gather(c, o):
        r = pl.ds(pl.multiple_of(c * R, R), R)
        return pltpu.make_async_remote_copy(
            src_ref=x.at[r, :], dst_ref=xg.at[b, r, :], send_sem=x_send.at[c, o - 1], recv_sem=x_recv.at[c, o - 1],
            device_id=(dp, a, peer(o)), device_id_type=mesh_id)

    def loads(c):
        slot = lax.rem(c, 2)
        out = []
        for o in range(nb):
            for k in range(2):
                side = 1 - a if k == 0 else a
                r = pl.ds(pl.multiple_of(c * R + side * half, half), half)
                src = x.at[r, :] if o == 0 else xg.at[peer(o), r, :]
                cols = pl.ds(pl.multiple_of(peer(o) * xb, xb), xb)
                out.append(pltpu.make_async_copy(src, xv.at[slot, pl.ds(k * half, half), cols], x_load.at[o * 2 + k]))
        return out

    def weights(n):
        t = lax.rem(n, tiles)
        slot = lax.rem(n, WSLOTS)
        cols = pl.ds(pl.multiple_of(t * F, F), F)
        return (pltpu.make_async_copy(w_gate.at[:, cols], wg.at[slot], wg_sem.at[slot]),
                pltpu.make_async_copy(w_up.at[:, cols], wu.at[slot], wu_sem.at[slot]))

    def down_weights(q):
        slot = lax.rem(q, WSLOTS)
        j = lax.rem(q // GROUP, down_groups)
        i = lax.rem(q, GROUP)
        return pltpu.make_async_copy(
            w_down.at[pl.ds(pl.multiple_of(j * depth, depth), depth), pl.ds(pl.multiple_of(i * third, third), third)],
            wd.at[slot], wd_sem.at[slot])

    def partial(n):
        slot = lax.rem(n, SLOTS)
        return pltpu.make_async_remote_copy(
            src_ref=sent.at[slot], dst_ref=got.at[slot], send_sem=p_send.at[slot], recv_sem=p_recv.at[slot],
            device_id=partner, device_id_type=mesh_id)

    def hidden(m):
        slot = lax.rem(m // GROUP, HSLOTS)
        s = lax.rem(m, GROUP * HSLOTS)
        i = lax.rem(m, GROUP)
        cols = pl.ds(pl.multiple_of(i * F, F), F)
        return pltpu.make_async_remote_copy(
            src_ref=hid.at[slot, pl.ds(0, half), cols], dst_ref=hid.at[slot, pl.ds(half, half), cols],
            send_sem=h_send.at[s], recv_sem=h_recv.at[s], device_id=partner, device_id_type=mesh_id)

    def reduce(c, o):
        slot = lax.rem(c, 2)
        return pltpu.make_async_remote_copy(
            src_ref=rsent.at[o - 1], dst_ref=rgot.at[slot, o - 1], send_sem=r_send.at[o - 1],
            recv_sem=r_recv.at[slot, o - 1], device_id=(dp, a, peer(o)), device_id_type=mesh_id)

    def stores(c):
        out = []
        for k in range(2):
            side = a if k == 0 else 1 - a
            r = pl.ds(pl.multiple_of(c * R + side * half, half), half)
            out.append(pltpu.make_async_copy(yout.at[pl.ds(k * half, half), :], y.at[r, :], y_sem.at[k]))
        return out

    def finish(c):
        slot = lax.rem(c, 2)
        for o in range(1, nb):
            reduce(c, o).wait()

        @pl.when(c > 0)
        def _():
            for copy in stores(c - 1):
                copy.wait()

        for k in range(xb // sub):
            cols = pl.ds(k * sub, sub)
            total = own[k]
            for o in range(1, nb):
                total = total + rgot[slot, o - 1, :, cols].astype(jnp.float32)
            yout[:, cols] = total.astype(yout.dtype)
        for copy in stores(c):
            copy.start()

    barrier = pltpu.get_barrier_semaphore()
    for target in [partner] + [(dp, a, peer(o)) for o in range(1, nb)]:
        pl.semaphore_signal(barrier, inc=1, device_id=target, device_id_type=mesh_id)
    pl.semaphore_wait(barrier, nb)

    for o in (2, 3, 1):
        gather(0, o).start()
    for d in range(WSLOTS - 1):
        for copy in weights(d):
            copy.start()
    acc[...] = jnp.zeros_like(acc)
    for o in range(1, nb):
        gather(0, o).wait()
    for o in range(1, nb):
        if chunks > 1:
            gather(1, o).start()
    for copy in loads(0):
        copy.start()

    def step(n, _):
        c = n // tiles
        t = lax.rem(n, tiles)
        live = n < steps
        m = n - LAG_HIDDEN
        q = n - LAG_DOWN

        ahead = n + WSLOTS - 1

        @pl.when(ahead < steps)
        def _():
            for copy in weights(ahead):
                copy.start()

        @pl.when((ahead >= LAG_DOWN) & (ahead - LAG_DOWN < steps))
        def _():
            down_weights(ahead - LAG_DOWN).start()

        @pl.when(live & (t == 0))
        def _():
            for copy in loads(c):
                copy.wait()

        @pl.when(live & (t == 1) & (c + 2 < chunks))
        def _():
            for o in (2, 3, 1):
                gather(c + 2, o).start()

        @pl.when(live & (t == tiles // 2) & (c + 1 < chunks))
        def _():
            for o in range(1, nb):
                gather(c + 1, o).wait()
            for copy in loads(c + 1):
                copy.start()

        @pl.when((n >= SLOTS) & (n - SLOTS < steps))
        def _():
            partial(n - SLOTS).wait_send()

        @pl.when(live)
        def _():
            for copy in weights(n):
                copy.wait()
            slot = lax.rem(n, SLOTS)
            ws = lax.rem(n, WSLOTS)
            xs = lax.rem(c, 2)
            for k, w in enumerate((wg, wu)):
                v = jnp.dot(xv[xs], w[ws], preferred_element_type=jnp.float32)
                sent[slot, k] = v[:half].astype(sent.dtype)
                keep[slot, k] = v[half:]
            partial(n).start()

        old = m - GROUP * HSLOTS

        @pl.when((old >= 0) & (old < steps))
        def _():
            hidden(old).wait_send()

        @pl.when((m >= 0) & (m < steps))
        def _():
            partial(m).wait_recv()
            slot = lax.rem(m, SLOTS)
            g = keep[slot, 0] + got[slot, 0].astype(jnp.float32)
            u = keep[slot, 1] + got[slot, 1].astype(jnp.float32)
            cols = pl.ds(pl.multiple_of(lax.rem(m, GROUP) * F, F), F)
            hid[lax.rem(m // GROUP, HSLOTS), pl.ds(0, half), cols] = (jax.nn.silu(g) * u).astype(hid.dtype)
            hidden(m).start()

        @pl.when((q >= 0) & (q < steps))
        def _():
            i = lax.rem(q, GROUP)

            @pl.when(i == 0)
            def _():
                for d in range(GROUP):
                    hidden(q + d).wait_recv()

            down_weights(q).wait()
            hs = lax.rem(q // GROUP, HSLOTS)
            ws = lax.rem(q, WSLOTS)
            for k in range(third // sub):
                v = jnp.dot(hid[hs], wd[ws, :, pl.ds(k * sub, sub)], preferred_element_type=jnp.float32)
                at = i * (third // sub) + k
                acc[at] = acc[at] + v

            cq = q // tiles

            @pl.when(lax.rem(q, tiles) == tiles - 1)
            def _():
                per = xb // sub
                for o in (2, 3, 1):
                    for k in range(per):
                        rsent[o - 1, :, pl.ds(k * sub, sub)] = acc[peer(o) * per + k].astype(rsent.dtype)
                    reduce(cq, o).start()
                for k in range(per):
                    own[k] = acc[b * per + k]
                acc[...] = jnp.zeros_like(acc)

        late = q - lag_sum

        @pl.when((late >= 0) & (lax.rem(late, tiles) == tiles - 1) & (late < steps - 1))
        def _():
            finish(late // tiles)

        return 0

    lax.fori_loop(0, steps + LAG_HIDDEN + GROUP * HSLOTS, step, 0)
    finish(chunks - 1)
    for copy in stores(chunks - 1):
        copy.wait()


def mlp(x, w_gate, w_up, w_down):
    rows, xb = x.shape
    kd, ff = w_gate.shape
    dn = w_down.shape[1]
    sub = dn // 12
    third = dn // GROUP
    bf, f32 = jnp.bfloat16, jnp.float32
    chunks = rows // R
    dma = pltpu.SemaphoreType.DMA
    any_spec = pl.BlockSpec(memory_space=pl.ANY)
    out, _ = pl.pallas_call(
        kernel,
        out_shape=(jax.ShapeDtypeStruct((rows, xb), bf), jax.ShapeDtypeStruct((4, rows, xb), bf)),
        in_specs=[any_spec] * 4,
        out_specs=(any_spec, any_spec),
        scratch_shapes=[
            pltpu.VMEM((2, R, kd), bf),
            pltpu.VMEM((WSLOTS, kd, F), bf),
            pltpu.VMEM((WSLOTS, kd, F), bf),
            pltpu.VMEM((WSLOTS, F * GROUP, third), bf),
            pltpu.VMEM((12, R, sub), f32),
            pltpu.VMEM((xb // sub, R, sub), f32),
            pltpu.VMEM((SLOTS, 2, R // 2, F), f32),
            pltpu.VMEM((SLOTS, 2, R // 2, F), bf),
            pltpu.VMEM((SLOTS, 2, R // 2, F), bf),
            pltpu.VMEM((HSLOTS, R, F * GROUP), bf),
            pltpu.VMEM((3, R, xb), bf),
            pltpu.VMEM((2, 3, R, xb), bf),
            pltpu.VMEM((R, xb), bf),
            dma((chunks, 3)), dma((chunks, 3)), dma((8,)),
            dma((WSLOTS,)), dma((WSLOTS,)), dma((WSLOTS,)),
            dma((SLOTS,)), dma((SLOTS,)),
            dma((GROUP * HSLOTS,)), dma((GROUP * HSLOTS,)),
            dma((3,)), dma((2, 3)), dma((2,)),
        ],
        compiler_params=pltpu.CompilerParams(collective_id=0, has_side_effects=True, vmem_limit_bytes=VMEM_LIMIT),
        cost_estimate=pl.CostEstimate(flops=6 * rows * kd * ff, bytes_accessed=3 * chunks * kd * ff * 2,
                                      transcendentals=rows * ff),
    )(x, w_gate, w_up, w_down)
    return out


def solution(mesh):
    return jax.shard_map(mlp, mesh=mesh, in_specs=(P("dp", ("a", "b")), P("a", "b"), P("a", "b"), P("b", "a")),
                         out_specs=P("dp", ("a", "b")), check_vma=False)
```

time: 2530 us -> 1210 us (0.48)
  waiting for transfers between devices: 1830 us -> 0 us
  Pallas kernels: 0 us -> 1200 us
  matrix products: 694 us -> 0 us
    dot_general x1 -> x0, waiting for transfers between devices: 1500 us -> none  [step(): gate, up = (jnp.dot(x, w_gate), jnp.dot(x, w_up))]
    pallas_call x0 -> x1, Pallas kernels: none -> 1200 us  [mlp(): pl.pallas_call(kernel, out_shape=(jax.ShapeDtypeStruct((rows, xb), bf), j...]
    dot_general x3 -> x0, matrix products: 694 us -> none  [the longest x2 452 us: step(): gate, up = (jnp.dot(x, w_gate), jnp.dot(x, w_up))]
    unnamed x5 -> x0, waiting for transfers between devices: 329 us -> none
  transfers between devices with their start and end apart: 3 -> 0, of which waited for: 3 -> 0; matrix products, arithmetic and copies ran while one was open for 0% -> 0% of each run, Pallas kernels for 0% -> 0%
where the time goes in v1:
time: 1210 us
  Pallas kernels  1200 us (99%)
    pallas_call x1, Pallas kernels, mlp(): pl.pallas_call(kernel, out_shape=(jax.ShapeDtypeStruct((rows, xb), bf), j...  1200 us

profile of v1, /device:TPU:0, one launch (start us, length us, event | category | flops | bytes accessed | tf_op | source)
XLA Modules:
  0.0 1205.7 jit_solution(14502260016452517989)
XLA Ops:
  0.0 1199.8 %shard_map.46 = (bf16[2048,1536]{1,0:T(8,128)(2,1)}, bf16[4,2048,1536]{2,1,0:T(8,128)(2,1)}) custom-call(bf16[2048,1536]{1,0:T(8,128)(2,1)} %x.1, bf16[6144,8448]{1,0:T(8,128)(2,1)} %w_gate.1, bf16[6144,8448]{1,0:T(8,128)(2,1)} %w_up.1, bf16[8448,6144]{1,0:T(8,128)(2,1)} %w_down.1), custom_call_target="tpu_custom_call" | custom-call | flops 637802643456 | bytes 2491416576 | tf_op jit(solution)/shard_map/pallas_call | solution.py:261
  1199.8 5.9 copy.6

commit v2 on v1

v2 whole, which is shorter than its diff:
```python
import functools
import jax
import jax.numpy as jnp
from jax import lax
from jax.experimental import pallas as pl
from jax.experimental.pallas import tpu as pltpu
from jax.sharding import PartitionSpec as P

R = 256
F = 256
GROUP = 3
LAG_HIDDEN = 4
LAG_DOWN = 12
SLOTS = LAG_DOWN + 2
HSLOTS = LAG_DOWN // GROUP + 1
WSLOTS = 3
VMEM_LIMIT = 66 * 1000 * 1000


def kernel(x, w_gate, w_up, w_down, y, xg, xv, wg, wu, wd, acc, own, keep, sent, got, hid, rsent, rgot, yout,
           x_send, x_recv, x_load, wg_sem, wu_sem, wd_sem, p_send, p_recv, h_send, h_recv, r_send, r_recv, y_sem):
    dp, a, b = lax.axis_index("dp"), lax.axis_index("a"), lax.axis_index("b")
    nb = 4
    half = R // 2
    rows, xb = x.shape
    ff, dn = w_down.shape
    chunks, tiles = rows // R, ff // F
    steps = chunks * tiles
    third, sub = dn // GROUP, acc.shape[2]
    per = xb // sub
    places = third // sub
    depth = F * GROUP
    down_groups = tiles // GROUP
    lag_sum = tiles // 2
    mesh_id = pltpu.DeviceIdType.MESH if hasattr(pltpu, "DeviceIdType") else pl.DeviceIdType.MESH
    partner = (dp, 1 - a, b)

    sibling = b + 1 - 2 * lax.rem(b, 2)
    across = lax.rem(b + 2, nb)
    diagonal = lax.rem(sibling + 2, nb)
    owners = (b, sibling, across, diagonal)

    def half_rows(c, k):
        side = 1 - a if k == 0 else a
        return pl.ds(pl.multiple_of(c * R + side * half, half), half)

    def gather(c, kind, k):
        r = half_rows(c, k)
        owner = across if kind == 2 else b
        return pltpu.make_async_remote_copy(
            src_ref=xg.at[owner, r, :] if kind == 2 else x.at[r, :], dst_ref=xg.at[owner, r, :],
            send_sem=x_send.at[c, kind, k], recv_sem=x_recv.at[c, kind, k],
            device_id=(dp, a, across if kind == 1 else sibling), device_id_type=mesh_id)

    def first(kind, k):
        owner = across if kind == 2 else b
        cols = pl.ds(pl.multiple_of(owner * xb, xb), xb)
        dst = xv.at[0, pl.ds(k * half, half), cols]
        return pltpu.make_async_remote_copy(
            src_ref=dst if kind == 2 else x.at[half_rows(0, k), :], dst_ref=dst,
            send_sem=x_send.at[0, kind, k], recv_sem=x_recv.at[0, kind, k],
            device_id=(dp, a, across if kind == 1 else sibling), device_id_type=mesh_id)

    def load(c, o, k):
        r = half_rows(c, k)
        src = x.at[r, :] if o == 0 else xg.at[owners[o], r, :]
        cols = pl.ds(pl.multiple_of(owners[o] * xb, xb), xb)
        return pltpu.make_async_copy(src, xv.at[lax.rem(c, 2), pl.ds(k * half, half), cols], x_load.at[o, k])

    def weights(n):
        t = lax.rem(n, tiles)
        slot = lax.rem(n, WSLOTS)
        cols = pl.ds(pl.multiple_of(t * F, F), F)
        return (pltpu.make_async_copy(w_gate.at[:, cols], wg.at[slot], wg_sem.at[slot]),
                pltpu.make_async_copy(w_up.at[:, cols], wu.at[slot], wu_sem.at[slot]))

    def owner_at(p):
        e = p // per
        return 2 * lax.rem(b // 2 + 1 - e // 2, 2) + lax.rem(lax.rem(b, 2) + 1 - lax.rem(e, 2), 2)

    def down_weights(q, slot):
        j = lax.rem(q // GROUP, down_groups)
        i = lax.rem(q, GROUP)
        r = pl.ds(pl.multiple_of(j * depth, depth), depth)
        out = []
        for k in range(places):
            p = i * places + k
            at = owner_at(p) * per + lax.rem(p, per)
            out.append(pltpu.make_async_copy(
                w_down.at[r, pl.ds(pl.multiple_of(at * sub, sub), sub)], wd.at[slot, k], wd_sem.at[slot, k]))
        return out

    def partial(n):
        slot = lax.rem(n, SLOTS)
        return pltpu.make_async_remote_copy(
            src_ref=sent.at[slot], dst_ref=got.at[slot], send_sem=p_send.at[slot], recv_sem=p_recv.at[slot],
            device_id=partner, device_id_type=mesh_id)

    def hidden(m):
        slot = lax.rem(m // GROUP, HSLOTS)
        s = lax.rem(m, GROUP * HSLOTS)
        i = lax.rem(m, GROUP)
        cols = pl.ds(pl.multiple_of(i * F, F), F)
        return pltpu.make_async_remote_copy(
            src_ref=hid.at[slot, pl.ds(0, half), cols], dst_ref=hid.at[slot, pl.ds(half, half), cols],
            send_sem=h_send.at[s], recv_sem=h_recv.at[s], device_id=partner, device_id_type=mesh_id)

    own_rows, partner_rows, all_rows = pl.ds(0, half), pl.ds(half, half), pl.ds(0, R)

    def reduce(c, kind, k, r=all_rows, s=0):
        slot = lax.rem(c, 2)
        return pltpu.make_async_remote_copy(
            src_ref=rsent.at[kind, k, r], dst_ref=rgot.at[slot, kind, k, r], send_sem=r_send.at[kind, k, s],
            recv_sem=r_recv.at[slot, kind, k, s], device_id=(dp, a, across if kind == 2 else sibling),
            device_id_type=mesh_id)

    def stores(c, k, sides=(0, 1)):
        cols = pl.ds(k * sub, sub)
        return [pltpu.make_async_copy(yout.at[pl.ds(s * half, half), cols], y.at[half_rows(c, 1 - s), cols],
                                      y_sem.at[s, k]) for s in sides]

    def combine(c, third_done, r=all_rows, s=0):
        slot = lax.rem(c, 2)
        for k in range(per):
            if third_done == 0:
                rsent[0, k, r] = acc[k, r].astype(rsent.dtype)
                reduce(c, 0, k, r, s).start()
            elif third_done == 1:
                reduce(c, 0, k, r, s).wait_recv()
                total = acc[per + k, r] + rgot[slot, 0, k, r].astype(jnp.float32)
                rsent[2, k, r] = total.astype(rsent.dtype)
                reduce(c, 2, k, r, s).start()
            else:
                rsent[1, k, r] = acc[2 * per + k, r].astype(rsent.dtype)
                reduce(c, 1, k, r, s).start()
                own[k, r] = acc[3 * per + k, r]

    def stored(c):
        for k in range(per):
            for copy in stores(c, k):
                copy.wait()

    def finish(c, r=all_rows, s=0, sides=(0, 1)):
        slot = lax.rem(c, 2)
        for k in range(per):
            reduce(c, 1, k, r, s).wait_recv()
            reduce(c, 2, k, r, s).wait_recv()
            total = own[k, r] + rgot[slot, 1, k, r].astype(jnp.float32) + rgot[slot, 2, k, r].astype(jnp.float32)
            yout[r, pl.ds(k * sub, sub)] = total.astype(yout.dtype)
            for copy in stores(c, k, sides):
                copy.start()
        for k in range(per):
            for kind in range(3):
                reduce(c, kind, k, r, s).wait_send()

    def activate(m):
        partial(m).wait_recv()
        slot = lax.rem(m, SLOTS)
        g = keep[slot, 0] + got[slot, 0].astype(jnp.float32)
        u = keep[slot, 1] + got[slot, 1].astype(jnp.float32)
        cols = pl.ds(pl.multiple_of(lax.rem(m, GROUP) * F, F), F)
        hid[lax.rem(m // GROUP, HSLOTS), pl.ds(0, half), cols] = (jax.nn.silu(g) * u).astype(hid.dtype)
        hidden(m).start()

    def down(q, ws, r=all_rows):
        i = lax.rem(q, GROUP)
        for copy in down_weights(q, ws):
            copy.wait()
        hs = lax.rem(q // GROUP, HSLOTS)
        for k in range(places):
            v = jnp.dot(hid[hs, r], wd[ws, k], preferred_element_type=jnp.float32)
            at = i * places + k
            acc[at, r] = acc[at, r] + v

    barrier = pltpu.get_barrier_semaphore()
    for target in (partner, (dp, a, sibling), (dp, a, across)):
        pl.semaphore_signal(barrier, inc=1, device_id=target, device_id_type=mesh_id)
    pl.semaphore_wait(barrier, 3)

    for k in range(2):
        first(1, k).start()
        first(0, k).start()
        load(0, 0, k).start()
    for d in range(WSLOTS):
        for copy in weights(d):
            copy.start()
    acc[...] = jnp.zeros_like(acc)
    for k in range(2):
        first(1, k).wait_recv()
        first(2, k).start()
        first(0, k).wait_recv()
        load(0, 0, k).wait()
        first(2, k).wait_recv()
        if k == 0:
            for d in range(WSLOTS):
                for copy in weights(d):
                    copy.wait()
                for i, w in enumerate((wg, wu)):
                    sent[d, i] = jnp.dot(xv[0, :half], w[d], preferred_element_type=jnp.float32).astype(sent.dtype)
                partial(d).start()
    for k in range(2):
        for kind in range(3):
            first(kind, k).wait_send()
    for k in range(2):
        for kind in (1, 0):
            if chunks > 1:
                gather(1, kind, k).start()

    def step(n, _):
        c = n // tiles
        t = lax.rem(n, tiles)
        m = n - LAG_HIDDEN
        q = n - LAG_DOWN

        ahead = n + WSLOTS - 1

        @pl.when((ahead >= WSLOTS) & (ahead < steps))
        def _():
            for copy in weights(ahead):
                copy.start()

        @pl.when((ahead >= LAG_DOWN) & (ahead < steps + 2))
        def _():
            for copy in down_weights(ahead - LAG_DOWN, lax.rem(ahead - LAG_DOWN, WSLOTS)):
                copy.start()

        @pl.when((t == 0) & (c > 0))
        def _():
            for o in range(nb):
                for k in range(2):
                    load(c, o, k).wait()

        @pl.when((t == 1) & (c + 2 < chunks))
        def _():
            for k in range(2):
                for kind in (1, 0):
                    gather(c + 2, kind, k).start()

        @pl.when((t == tiles // 3) & (c + 1 < chunks))
        def _():
            for k in range(2):
                gather(c + 1, 1, k).wait_recv()
                gather(c + 1, 2, k).start()

        @pl.when((t == 2 * tiles // 3) & (c + 1 < chunks))
        def _():
            for k in range(2):
                gather(c + 1, 0, k).wait_recv()
                gather(c + 1, 2, k).wait_recv()
                for o in range(nb):
                    load(c + 1, o, k).start()
                for kind in range(3):
                    gather(c + 1, kind, k).wait_send()

        @pl.when(n >= SLOTS)
        def _():
            partial(n - SLOTS).wait_send()

        @pl.when(n < WSLOTS)
        def _():
            for k, w in enumerate((wg, wu)):
                keep[n, k] = jnp.dot(xv[0, half:], w[n], preferred_element_type=jnp.float32)

        @pl.when(n >= WSLOTS)
        def _():
            for copy in weights(n):
                copy.wait()
            slot = lax.rem(n, SLOTS)
            ws = lax.rem(n, WSLOTS)
            xs = lax.rem(c, 2)
            for k, w in enumerate((wg, wu)):
                v = jnp.dot(xv[xs], w[ws], preferred_element_type=jnp.float32)
                sent[slot, k] = v[:half].astype(sent.dtype)
                keep[slot, k] = v[half:]
            partial(n).start()

        old = m - GROUP * HSLOTS

        @pl.when(old >= 0)
        def _():
            hidden(old).wait_send()

        @pl.when(m >= 0)
        def _():
            activate(m)

        @pl.when(q >= 0)
        def _():
            @pl.when(lax.rem(q, GROUP) == 0)
            def _():
                for d in range(GROUP):
                    hidden(q + d).wait_recv()

            down(q, lax.rem(q, WSLOTS))
            cq, tq = q // tiles, lax.rem(q, tiles)
            for i in range(GROUP):
                @pl.when(tq == tiles - GROUP + i)
                def _():
                    combine(cq, i)
                    if i == GROUP - 1:
                        acc[...] = jnp.zeros_like(acc)

        late = q - lag_sum

        @pl.when((late >= 0) & (lax.rem(late, tiles) == tiles - 1))
        def _():
            @pl.when(late // tiles > 0)
            def _():
                stored(late // tiles - 1)

            finish(late // tiles)

        return 0

    lax.fori_loop(0, steps, step, 0)

    last = chunks - 1
    stored(last - 1)
    end = [(q, all_rows) for q in range(steps - 12, steps - 6)]
    end += [(q, own_rows) for q in range(steps - 6, steps)] + [(q, partner_rows) for q in range(steps - 6, steps)]
    for e, (q, r) in enumerate(end):
        if e % GROUP == 0 and e // GROUP < LAG_HIDDEN:
            m = steps - LAG_HIDDEN + e // GROUP
            hidden(m - GROUP * HSLOTS).wait_send()
            activate(m)
        if e + 2 < len(end):
            for copy in down_weights(end[e + 2][0], (steps - 12 + e + 2) % WSLOTS):
                copy.start()
        if q % GROUP == 0 and r is not own_rows:
            for d in range(GROUP):
                hidden(q + d).wait_recv()
        down(q, (steps - 12 + e) % WSLOTS, r)
        if q >= steps - GROUP:
            combine(last, q % GROUP, r, 0 if r is own_rows else 1)
    finish(last, own_rows, 0, (0,))
    finish(last, partner_rows, 1, (1,))
    for d in range(SLOTS):
        partial(steps - SLOTS + d).wait_send()
    for d in range(GROUP * HSLOTS):
        hidden(steps - GROUP * HSLOTS + d).wait_send()
    stored(last)


def mlp(x, w_gate, w_up, w_down):
    rows, xb = x.shape
    kd, ff = w_gate.shape
    dn = w_down.shape[1]
    sub = dn // 12
    third = dn // GROUP
    bf, f32 = jnp.bfloat16, jnp.float32
    chunks = rows // R
    dma = pltpu.SemaphoreType.DMA
    any_spec = pl.BlockSpec(memory_space=pl.ANY)
    out, _ = pl.pallas_call(
        kernel,
        out_shape=(jax.ShapeDtypeStruct((rows, xb), bf), jax.ShapeDtypeStruct((4, rows, xb), bf)),
        in_specs=[any_spec] * 4,
        out_specs=(any_spec, any_spec),
        scratch_shapes=[
            pltpu.VMEM((2, R, kd), bf),
            pltpu.VMEM((WSLOTS, kd, F), bf),
            pltpu.VMEM((WSLOTS, kd, F), bf),
            pltpu.VMEM((WSLOTS, third // sub, F * GROUP, sub), bf),
            pltpu.VMEM((12, R, sub), f32),
            pltpu.VMEM((xb // sub, R, sub), f32),
            pltpu.VMEM((SLOTS, 2, R // 2, F), f32),
            pltpu.VMEM((SLOTS, 2, R // 2, F), bf),
            pltpu.VMEM((SLOTS, 2, R // 2, F), bf),
            pltpu.VMEM((HSLOTS, R, F * GROUP), bf),
            pltpu.VMEM((3, xb // sub, R, sub), bf),
            pltpu.VMEM((2, 3, xb // sub, R, sub), bf),
            pltpu.VMEM((R, xb), bf),
            dma((chunks, 3, 2)), dma((chunks, 3, 2)), dma((4, 2)),
            dma((WSLOTS,)), dma((WSLOTS,)), dma((WSLOTS, third // sub)),
            dma((SLOTS,)), dma((SLOTS,)),
            dma((GROUP * HSLOTS,)), dma((GROUP * HSLOTS,)),
            dma((3, xb // sub, 2)), dma((2, 3, xb // sub, 2)), dma((2, xb // sub)),
        ],
        compiler_params=pltpu.CompilerParams(collective_id=0, has_side_effects=True, vmem_limit_bytes=VMEM_LIMIT),
        cost_estimate=pl.CostEstimate(flops=6 * rows * kd * ff, bytes_accessed=3 * chunks * kd * ff * 2,
                                      transcendentals=rows * ff),
    )(x, w_gate, w_up, w_down)
    return out


def solution(mesh):
    return jax.shard_map(mlp, mesh=mesh, in_specs=(P("dp", ("a", "b")), P("a", "b"), P("a", "b"), P("b", "a")),
                         out_specs=P("dp", ("a", "b")), check_vma=False)
```

time: 1210 us -> 1160 us (0.959)
  Pallas kernels: 1200 us -> 1150 us
    pallas_call x1, Pallas kernels: 1200 us -> 1150 us  [mlp(): pl.pallas_call(kernel, out_shape=(jax.ShapeDtypeStruct((rows, xb), bf), j...]
where the time goes in v2:
time: 1160 us
  Pallas kernels  1150 us (99%)
    pallas_call x1, Pallas kernels, mlp(): pl.pallas_call(kernel, out_shape=(jax.ShapeDtypeStruct((rows, xb), bf), j...  1150 us

profile of v2, /device:TPU:0, one launch (start us, length us, event | category | flops | bytes accessed | tf_op | source)
XLA Modules:
  0.0 1158.1 jit_solution(12046682182771819201)
XLA Ops:
  0.0 1152.2 %shard_map.46 = (bf16[2048,1536]{1,0:T(8,128)(2,1)}, bf16[4,2048,1536]{2,1,0:T(8,128)(2,1)}) custom-call(bf16[2048,1536]{1,0:T(8,128)(2,1)} %x.1, bf16[6144,8448]{1,0:T(8,128)(2,1)} %w_gate.1, bf16[6144,8448]{1,0:T(8,128)(2,1)} %w_up.1, bf16[8448,6144]{1,0:T(8,128)(2,1)} %w_down.1), custom_call_target="tpu_custom_call" | custom-call | flops 637802643456 | bytes 2491416576 | tf_op jit(solution)/shard_map/pallas_call | solution.py:354
  1152.2 5.9 copy.6

commit v3 on v2

--- a/solution.py
+++ b/solution.py
@@ -67,9 +67,8 @@
         cols = pl.ds(pl.multiple_of(owners[o] * xb, xb), xb)
         return pltpu.make_async_copy(src, xv.at[lax.rem(c, 2), pl.ds(k * half, half), cols], x_load.at[o, k])
 
-    def weights(n):
+    def weights(n, slot):
         t = lax.rem(n, tiles)
-        slot = lax.rem(n, WSLOTS)
         cols = pl.ds(pl.multiple_of(t * F, F), F)
         return (pltpu.make_async_copy(w_gate.at[:, cols], wg.at[slot], wg_sem.at[slot]),
                 pltpu.make_async_copy(w_up.at[:, cols], wu.at[slot], wu_sem.at[slot]))
@@ -95,6 +94,16 @@
         return pltpu.make_async_remote_copy(
             src_ref=sent.at[slot], dst_ref=got.at[slot], send_sem=p_send.at[slot], recv_sem=p_recv.at[slot],
             device_id=partner, device_id_type=mesh_id)
+
+    def send_and_keep(n, ws, xs):
+        for copy in weights(n, ws):
+            copy.wait()
+        slot = lax.rem(n, SLOTS)
+        for k, w in enumerate((wg, wu)):
+            v = jnp.dot(xv[xs], w[ws], preferred_element_type=jnp.float32)
+            sent[slot, k] = v[:half].astype(sent.dtype)
+            keep[slot, k] = v[half:]
+        partial(n).start()
 
     def hidden(m):
         slot = lax.rem(m // GROUP, HSLOTS)
@@ -182,9 +191,19 @@
         first(0, k).start()
         load(0, 0, k).start()
     for d in range(WSLOTS):
-        for copy in weights(d):
+        for copy in weights(d, d):
             copy.start()
     acc[...] = jnp.zeros_like(acc)
+
+    start_steps = [d for d in range(WSLOTS)]
+    for d in range(WSLOTS):
+        start_steps += [WSLOTS + d, d]
+
+    def fetch(e):
+        n = start_steps[e] if e < len(start_steps) else e - WSLOTS
+        for copy in weights(n, e % WSLOTS):
+            copy.start()
+
     for k in range(2):
         first(1, k).wait_recv()
         first(2, k).start()
@@ -193,11 +212,12 @@
         first(2, k).wait_recv()
         if k == 0:
             for d in range(WSLOTS):
-                for copy in weights(d):
+                for copy in weights(d, d):
                     copy.wait()
                 for i, w in enumerate((wg, wu)):
                     sent[d, i] = jnp.dot(xv[0, :half], w[d], preferred_element_type=jnp.float32).astype(sent.dtype)
                 partial(d).start()
+                fetch(WSLOTS + d)
     for k in range(2):
         for kind in range(3):
             first(kind, k).wait_send()
@@ -206,6 +226,25 @@
             if chunks > 1:
                 gather(1, kind, k).start()
 
+    for e in range(WSLOTS, len(start_steps)):
+        n = start_steps[e]
+        if e > WSLOTS:
+            fetch(e + WSLOTS - 1)
+        if n >= WSLOTS:
+            send_and_keep(n, e % WSLOTS, 0)
+        else:
+            for copy in weights(n, e % WSLOTS):
+                copy.wait()
+            for k, w in enumerate((wg, wu)):
+                keep[n, k] = jnp.dot(xv[0, half:], w[e % WSLOTS], preferred_element_type=jnp.float32)
+            m = n + WSLOTS - LAG_HIDDEN
+            if m >= 0:
+                activate(m)
+    for k in range(2):
+        for kind in (1, 0):
+            if chunks > 2:
+                gather(2, kind, k).start()
+
     def step(n, _):
         c = n // tiles
         t = lax.rem(n, tiles)
@@ -214,9 +253,9 @@
 
         ahead = n + WSLOTS - 1
 
-        @pl.when((ahead >= WSLOTS) & (ahead < steps))
-        def _():
-            for copy in weights(ahead):
+        @pl.when(ahead < steps)
+        def _():
+            for copy in weights(ahead, lax.rem(ahead, WSLOTS)):
                 copy.start()
 
         @pl.when((ahead >= LAG_DOWN) & (ahead < steps + 2))
@@ -256,23 +295,7 @@
         def _():
             partial(n - SLOTS).wait_send()
 
-        @pl.when(n < WSLOTS)
-        def _():
-            for k, w in enumerate((wg, wu)):
-                keep[n, k] = jnp.dot(xv[0, half:], w[n], preferred_element_type=jnp.float32)
-
-        @pl.when(n >= WSLOTS)
-        def _():
-            for copy in weights(n):
-                copy.wait()
-            slot = lax.rem(n, SLOTS)
-            ws = lax.rem(n, WSLOTS)
-            xs = lax.rem(c, 2)
-            for k, w in enumerate((wg, wu)):
-                v = jnp.dot(xv[xs], w[ws], preferred_element_type=jnp.float32)
-                sent[slot, k] = v[:half].astype(sent.dtype)
-                keep[slot, k] = v[half:]
-            partial(n).start()
+        send_and_keep(n, lax.rem(n, WSLOTS), lax.rem(c, 2))
 
         old = m - GROUP * HSLOTS
 
@@ -280,9 +303,7 @@
         def _():
             hidden(old).wait_send()
 
-        @pl.when(m >= 0)
-        def _():
-            activate(m)
+        activate(m)
 
         @pl.when(q >= 0)
         def _():
@@ -312,7 +333,7 @@
 
         return 0
 
-    lax.fori_loop(0, steps, step, 0)
+    lax.fori_loop(2 * WSLOTS, steps, step, 0)
 
     last = chunks - 1
     stored(last - 1)

time: 1160 us -> 1150 us (level)
  no operation moved by 1% of the time
where the time goes in v3:
time: 1150 us
  Pallas kernels  1150 us (100%)
    pallas_call x1, Pallas kernels, mlp(): pl.pallas_call(kernel, out_shape=(jax.ShapeDtypeStruct((rows, xb), bf), j...  1150 us

profile of v3, /device:TPU:0, one launch (start us, length us, event | category | flops | bytes accessed | tf_op | source)
XLA Modules:
  0.0 1154.0 jit_solution(14754631128041873803)
XLA Ops:
  0.0 1148.1 %shard_map.46 = (bf16[2048,1536]{1,0:T(8,128)(2,1)}, bf16[4,2048,1536]{2,1,0:T(8,128)(2,1)}) custom-call(bf16[2048,1536]{1,0:T(8,128)(2,1)} %x.1, bf16[6144,8448]{1,0:T(8,128)(2,1)} %w_gate.1, bf16[6144,8448]{1,0:T(8,128)(2,1)} %w_up.1, bf16[8448,6144]{1,0:T(8,128)(2,1)} %w_down.1), custom_call_target="tpu_custom_call" | custom-call | flops 637802643456 | bytes 2491416576 | tf_op jit(solution)/shard_map/pallas_call | solution.py:375
  1148.2 5.9 copy.6
